TPU v7x, 32 devices: a whole 2x2x4 slice. The times are simulated.
32 devices in a mesh: dp: 8 (over y, x, core), tensor: 4 (over z).
Axes of the slice: x: 2, y: 2, z: 4, core: 2. Of those that a mesh axis runs over, the one named last changes fastest.
Arguments:
- tokens: bfloat16 [256, 6144], P('dp', 'tensor'), may hold values from -6 to 6
- router_weight: bfloat16 [6144, 8], P('tensor'), may hold values from -0.078125 to 0.078125
- expert_ids: int32 [256, 2], P('dp'), may hold values from 0 to 7, all different within a row; in each aligned block of 32 rows (0 to 31, 32 to 63, ...) at most 12 rows name the same one
- w_gate: bfloat16 [8, 6144, 12288], P('dp', None, 'tensor'), may hold values from -0.078125 to 0.078125
- w_up: bfloat16 [8, 6144, 12288], P('dp', None, 'tensor'), may hold values from -0.078125 to 0.078125
- w_down: bfloat16 [8, 12288, 6144], P('dp', 'tensor'), may hold values from -0.0546875 to 0.0546875
Outputs:
- moe_out: bfloat16 [256, 6144], P('dp', 'tensor')
Inputs may be any that keep to these rules, and one draw needn't show every extreme that they name: `expert_ids`: the two experts of a token differ. In each aligned block of 32 rows (the rows of one index of dp) no expert is named by more than 12 rows, a bound that some blocks reach.
All inputs are finite; a program needn't handle non-finite values.
Results may differ from a plain program's by a relative error of at most 0.022.
Values may be sent and summed in bfloat16 or wider, within the bound.
A program may use at most 192 MiB of HBM per device.

v0:
```python
import jax
import jax.numpy as jnp
from jax import lax
from jax.sharding import PartitionSpec as P

EXPERTS = 8
CAP = 12


def per_device(tokens, router_weight, expert_ids, w_gate, w_up, w_down):
    tok_rows = tokens.shape[0]
    share = tokens.shape[1]
    dp_count = lax.axis_size("dp")
    groups = dp_count // EXPERTS
    slot_count = EXPERTS * CAP
    partial_value = jnp.dot(tokens, router_weight, preferred_element_type=jnp.float32)
    logits = lax.psum(partial_value, "tensor")
    choose = (expert_ids[:, :, None] == jnp.arange(EXPERTS, dtype=jnp.int32)[None, None, :]).astype(
        jnp.float32
    )
    chosen = jnp.sum(choose * logits[:, None, :], axis=2)
    first = jax.nn.sigmoid(chosen[:, 0] - chosen[:, 1])
    gates = jnp.stack([first, 1.0 - first], axis=1)
    flat = expert_ids.reshape(-1)
    onehot = (flat[:, None] == jnp.arange(EXPERTS, dtype=jnp.int32)[None, :]).astype(jnp.int32)
    ranks = jnp.sum((jnp.cumsum(onehot, axis=0) - onehot) * onehot, axis=1)
    position = flat * CAP + ranks
    slot_table = (position[:, None] == jnp.arange(slot_count, dtype=jnp.int32)[None, :]).astype(
        jnp.float32
    )
    slot_table = slot_table.reshape(tok_rows, 2, slot_count)
    placing = jnp.sum(slot_table, axis=1).astype(jnp.bfloat16)
    weights = jnp.sum(slot_table * gates[:, :, None], axis=1)
    packed = lax.dot_general(
        placing, tokens, (((0,), (0,)), ((), ())), preferred_element_type=jnp.float32
    ).astype(jnp.bfloat16)
    outgoing = jnp.broadcast_to(
        packed.reshape(EXPERTS, 1, CAP, share), (EXPERTS, groups, CAP, share)
    ).reshape(dp_count, CAP, share)
    incoming = lax.all_to_all(outgoing, "dp", split_axis=0, concat_axis=0, tiled=True)
    rows = incoming.reshape(dp_count * CAP, share)
    gate_w = w_gate[0]
    up_w = w_up[0]
    down_w = w_down[0]
    whole = lax.all_gather(rows, "tensor", axis=1, tiled=True)
    gate = jnp.dot(whole, gate_w, preferred_element_type=jnp.float32)
    up = jnp.dot(whole, up_w, preferred_element_type=jnp.float32)
    hidden = (jax.nn.silu(gate) * up).astype(jnp.bfloat16)
    terms = jnp.dot(hidden, down_w, preferred_element_type=jnp.float32)
    summed = lax.psum_scatter(terms.astype(jnp.bfloat16), "tensor", scatter_dimension=1, tiled=True)
    leaving = summed.reshape(dp_count, CAP, share)
    back = lax.all_to_all(leaving, "dp", split_axis=0, concat_axis=0, tiled=True)
    merged = jnp.sum(back.astype(jnp.float32).reshape(EXPERTS, groups, CAP, share), axis=1).reshape(
        slot_count, share
    )
    result = jnp.dot(
        weights, merged, precision=lax.Precision.HIGHEST, preferred_element_type=jnp.float32
    )
    return result.astype(jnp.bfloat16)


def solution(mesh):
    return jax.shard_map(
        per_device,
        mesh=mesh,
        in_specs=(
            P("dp", "tensor"),
            P("tensor", None),
            P("dp", None),
            P("dp", None, "tensor"),
            P("dp", None, "tensor"),
            P("dp", "tensor", None),
        ),
        out_specs=P("dp", "tensor"),
        check_vma=False,
    )
```

profile of v0, /device:TPU:0, one launch (start us, length us, event | category | flops | bytes accessed | tf_op | source)
XLA Modules:
  0.0 160.2 jit_solution(1804313521024078486)
XLA Ops:
  6.5 0.0 copy-start
  6.5 0.0 all-gather.2.cloned.1.call-start
  6.5 0.9 copy-done
  7.4 0.9 fusion.21
  8.3 13.5 %psum.7 = f32[32,8]{0,1:T(8,128)S(1)} all-reduce(f32[32,8]{0,1:T(8,128)S(1)} %fusion.21), channel_id=1, replica_groups=mesh['dp'=8,'tensor'=4] {'tensor'}, use_global_device_ids=true, to_apply=%region_2.0 | all-reduce | flops 256 | bytes 2048 | tf_op jit(solution)/shard_map/psum | solution.py:17
  21.8 0.8 copy.27
  22.5 0.7 select_reduce_fusion.2
  23.2 0.1 eq.42
  23.3 0.1 fusion.18
  23.4 0.1 reduce_window_sum.11
  23.5 0.2 select_reduce_fusion.1
  23.7 0.1 reduce_sum.43
  23.8 0.1 copy.28
  23.9 0.7 multiply_add_fusion
  24.6 0.1 convert_reduce_fusion
  24.7 0.3 convolution_convert_fusion
  25.0 0.1 reshape_reshape.3
  25.0 11.8 %all_to_all.10 = bf16[8,12,1536]{2,1,0:T(8,128)(2,1)S(1)} all-to-all(bf16[8,12,1536]{2,1,0:T(8,128)(2,1)S(1)} %reshape_reshape.3), channel_id=1, replica_groups=mesh['dp'=8,'tensor'=4] {'dp'}, dimensions={0} | all-to-all | bytes 589824 | tf_op jit(solution)/shard_map/all_to_all | solution.py:40
  36.8 0.8 reshape.35
  37.6 0.0 all-gather.2.cloned.1.call-update
  37.7 0.0 reduce-scatter.2.cloned.1.call-start
  37.7 26.7 %all-gather.2.cloned.1.call-done = bf16[96,6144]{1,0:T(8,128)(2,1)} async-done(((bf16[96,1536]{1,0:T(8,128)(2,1)}), bf16[96,6144]{1,0:T(8,128)(2,1)}) %all-gather.2.cloned.1.call-update) | async-done | bytes 1179664 | tf_op jit(solution)/shard_map/all_gather | solution.py:45
  64.4 0.0 copy-start.2
  64.4 18.4 %fusion.4 = f32[96,3072]{1,0:T(8,128)S(1)} fusion(bf16[96,6144]{1,0:T(8,128)(2,1)} %all-gather.2.cloned.1.call-done, bf16[1,6144,3072]{2,1,0:T(8,128)(2,1)} %param.9), kind=kOutput, calls=%fused_computation.4 | convolution fusion | flops 3623878656 | bytes 40108032 | tf_op jit(solution)/shard_map/dot_general | solution.py:46
  82.8 0.0 copy-done.2
  82.8 28.1 %fusion.6 = bf16[96,6144]{1,0:T(8,128)(2,1)} fusion(bf16[1,3072,6144]{2,1,0:T(8,128)(2,1)} %param.11, bf16[96,6144]{1,0:T(8,128)(2,1)S(1)} %copy-done.2, bf16[1,6144,3072]{2,1,0:T(8,128)(2,1)} %param.10, f32[96,3072]{1,0:T(8,128)S(1)} %fusion.4), kind=kOutput, calls=%fused_computation.6 | convolution fusion | flops 7250116608 | bytes 79036416 | tf_op jit(solution)/shard_map/dot_general | solution.py:49
  110.9 0.0 reduce-scatter.2.cloned.1.call-update
  110.9 0.0 copy-start.1
  110.9 28.7 %reduce-scatter.2.cloned.1.call-done = bf16[96,1536]{1,0:T(8,128)(2,1)} async-done(((bf16[96,6144]{1,0:T(8,128)(2,1)}), bf16[96,1536]{1,0:T(8,128)(2,1)}) %reduce-scatter.2.cloned.1.call-update) | async-done | bytes 294928 | tf_op jit(solution)/shard_map/reduce_scatter | solution.py:50
  139.6 1.0 reshape.36
  140.7 11.8 %all_to_all.11 = bf16[8,12,1536]{2,1,0:T(8,128)(2,1)S(1)} all-to-all(bf16[8,12,1536]{2,1,0:T(8,128)(2,1)S(1)} %reshape.36), channel_id=1, replica_groups=mesh['dp'=8,'tensor'=4] {'dp'}, dimensions={0} | all-to-all | bytes 589824 | tf_op jit(solution)/shard_map/all_to_all | solution.py:52
  152.4 0.1 reshape.37
  152.5 0.9 convolution_convert_fusion.1
  153.4 0.0 copy-done.1
  (2 shorter events, 0.0 us)
Async XLA Ops:
  6.5 0.9 copy-start
  6.5 57.9 %all-gather.2.cloned.1.call-start = ((), (), s32[]{:S(2)}) async-start(), calls=%async_computation.3 | async-start | bytes 1474560 | tf_op jit(solution)/shard_map/all_gather | solution.py:45
  37.7 102.0 %reduce-scatter.2.cloned.1.call-start = ((), (), s32[]{:S(2)}) async-start(), calls=%async_computation.4 | async-start | bytes 1474560 | tf_op jit(solution)/shard_map/reduce_scatter | solution.py:50
  64.4 18.4 %copy-start.2 = (bf16[96,6144]{1,0:T(8,128)(2,1)S(1)}, bf16[96,6144]{1,0:T(8,128)(2,1)}, u32[]{:S(2)}) copy-start(bf16[96,6144]{1,0:T(8,128)(2,1)} %all-gather.2.cloned.1.call-done) | copy-start | bytes 3538948
  110.9 42.5 %copy-start.1 = (bf16[32,1536]{1,0:T(8,128)(2,1)S(1)}, bf16[32,1536]{1,0:T(8,128)(2,1)}, u32[]{:S(2)}) copy-start(bf16[32,1536]{1,0:T(8,128)(2,1)} %param.6) | copy-start | bytes 294916
Sparse Core Ops, SparseCore 0:
  37.8 26.5 all-gather.1
  111.0 28.5 reduce-scatter.1
where the time goes:
time: 161 us; the launch traced here: 160 us
  waiting for transfers between devices  55.4 us (34%)
  matrix products  48.5 us (30%)
  blocking collectives  37 us (23%)
  between operations  13.5 us (8%)
  local copies, waits for them, and re-layouts  3.9 us (2%)
  other arithmetic  1.85 us (1%)
    reduce_scatter x1, waiting for transfers between devices, per_device(): lax.psum_scatter(terms.astype(jnp.bfloat16), 'tensor', scatter_dimension=...  28.7 us
    dot_general x1, matrix products, per_device(): terms = jnp.dot(hidden, down_w, preferred_element_type=jnp.float32)  28.1 us
    all_gather x1, waiting for transfers between devices, per_device(): whole = lax.all_gather(rows, 'tensor', axis=1, tiled=True)  26.7 us
    dot_general x1, matrix products, per_device(): gate = jnp.dot(whole, gate_w, preferred_element_type=jnp.float32)  18.4 us
    psum x1, blocking collectives, per_device(): logits = lax.psum(partial_value, 'tensor')  13.5 us
    all_to_all x1, blocking collectives, per_device(): lax.all_to_all(outgoing, 'dp', split_axis=0, concat_axis=0, tiled=True)  11.8 us
    all_to_all x1, blocking collectives, per_device(): lax.all_to_all(leaving, 'dp', split_axis=0, concat_axis=0, tiled=True)  11.8 us
  transfers between devices with their start and end apart: 2, of which 2 were waited for; matrix products, arithmetic and copies ran while one was open for 0% of the time, Pallas kernels for 0%

commit v1 on v0

--- a/solution.py
+++ b/solution.py
@@ -37,7 +37,19 @@
     outgoing = jnp.broadcast_to(
         packed.reshape(EXPERTS, 1, CAP, share), (EXPERTS, groups, CAP, share)
     ).reshape(dp_count, CAP, share)
-    incoming = lax.all_to_all(outgoing, "dp", split_axis=0, concat_axis=0, tiled=True)
+    ways, here = (lax.axis_size("dp"), lax.axis_index("dp"))
+    width = outgoing.shape[0] // ways
+    dims = list(outgoing.shape)
+    dims[0] = width
+    height = dims[0]
+    dims[0] = height * ways
+    full = jnp.zeros(dims, outgoing.dtype)
+    for mask in range(ways):
+        part = lax.dynamic_slice_in_dim(outgoing, (here ^ mask) * width, width, axis=0)
+        if mask:
+            part = lax.ppermute(part, "dp", [(d, d ^ mask) for d in range(ways)])
+        full = lax.dynamic_update_slice_in_dim(full, part, (here ^ mask) * height, axis=0)
+    incoming = full
     rows = incoming.reshape(dp_count * CAP, share)
     gate_w = w_gate[0]
     up_w = w_up[0]

time: 161 us -> 163 us (1.012)
  blocking collectives: 37 us -> 25.2 us
  waiting for transfers between devices: 55.4 us -> 63 us
  starting transfers between devices: 0.04 us -> 6.72 us
    all_to_all x1 -> x0, blocking collectives: 11.8 us -> none  [per_device(): lax.all_to_all(outgoing, 'dp', split_axis=0, concat_axis=0, tiled=True)]
    ppermute x0 -> x7, starting transfers between devices: none -> 6.67 us  [per_device(): part = lax.ppermute(part, 'dp', [(d, d ^ mask) for d in range(ways)])]
    ppermute x0 -> x7, waiting for transfers between devices: none -> 6.04 us  [per_device(): part = lax.ppermute(part, 'dp', [(d, d ^ mask) for d in range(ways)])]
  transfers between devices with their start and end apart: 2 -> 9, of which waited for: 2 -> 4; matrix products, arithmetic and copies ran while one was open for 0% -> 0% of each run, Pallas kernels for 0% -> 0%
where the time goes in v1:
time: 163 us
  waiting for transfers between devices  63 us (39%)
  matrix products  48.3 us (30%)
  blocking collectives  25.2 us (15%)
  between operations  13.6 us (8%)
  starting transfers between devices  6.72 us (4%)
  local copies, waits for them, and re-layouts  4.04 us (2%)
  other arithmetic  1.85 us (1%)
    reduce_scatter x1, waiting for transfers between devices, per_device(): lax.psum_scatter(terms.astype(jnp.bfloat16), 'tensor', scatter_dimension=...  28.7 us
    all_gather x1, waiting for transfers between devices, per_device(): whole = lax.all_gather(rows, 'tensor', axis=1, tiled=True)  28.3 us
    dot_general x1, matrix products, per_device(): terms = jnp.dot(hidden, down_w, preferred_element_type=jnp.float32)  28.1 us
    dot_general x1, matrix products, per_device(): up = jnp.dot(whole, up_w, preferred_element_type=jnp.float32)  18.2 us
    psum x1, blocking collectives, per_device(): logits = lax.psum(partial_value, 'tensor')  13.5 us
    all_to_all x1, blocking collectives, per_device(): lax.all_to_all(leaving, 'dp', split_axis=0, concat_axis=0, tiled=True)  11.8 us
    ppermute x7, starting transfers between devices, per_device(): part = lax.ppermute(part, 'dp', [(d, d ^ mask) for d in range(ways)])  6.67 us
    ppermute x7, waiting for transfers between devices, per_device(): part = lax.ppermute(part, 'dp', [(d, d ^ mask) for d in range(ways)])  6.04 us
  transfers between devices with their start and end apart: 9, of which 4 were waited for; matrix products, arithmetic and copies ran while one was open for 0% of the time, Pallas kernels for 0%

profile of v1, /device:TPU:0, one launch (start us, length us, event | category | flops | bytes accessed | tf_op | source)
XLA Modules:
  0.0 162.8 jit_solution(7742500097044477660)
XLA Ops:
  6.5 0.0 copy-start
  6.5 0.0 all-gather.2.cloned.1.call-start
  6.5 0.9 copy-done
  7.4 0.9 fusion.17
  8.3 13.5 %psum.7 = f32[32,8]{0,1:T(8,128)S(1)} all-reduce(f32[32,8]{0,1:T(8,128)S(1)} %fusion.17), channel_id=1, replica_groups=mesh['dp'=8,'tensor'=4] {'tensor'}, use_global_device_ids=true, to_apply=%region_2.0 | all-reduce | flops 256 | bytes 2048 | tf_op jit(solution)/shard_map/psum | solution.py:17
  21.8 0.8 copy.27
  22.5 0.7 select_reduce_fusion.2
  23.2 0.1 eq.42
  23.3 0.1 fusion.14
  23.4 0.1 reduce_window_sum.11
  23.5 0.2 select_reduce_fusion.1
  23.7 0.1 reduce_sum.43
  23.8 0.1 copy.28
  23.9 0.7 multiply_add_fusion
  24.6 0.1 convert_reduce_fusion
  24.7 0.3 convolution_convert_fusion
  25.0 0.1 reshape_reshape.3
  25.2 0.1 collective-permute-start
  25.2 2.5 %collective-permute-start.6 = (bf16[1,12,1536]{2,1,0:T(8,128)(2,1)S(1)}, bf16[1,12,1536]{2,1,0:T(8,128)(2,1)S(1)}, u32[]{:S(2)}, u32[]{:S(2)}) collective-permute-start(bf16[1,12,1536]{2,1,0:T(8,128)(2,1)S(1)} %get-tuple-element.9), channel_id=1, source_target_pairs={{0,28},{4,24},{8,20},{12,16},{16,12},{20,8},{24,4},{28,0},{1,29},{... | collective-permute-start | bytes 110600 | tf_op jit(solution)/shard_map/ppermute | solution.py:50
  27.8 0.5 collective-permute-start.5
  28.3 0.9 collective-permute-start.4
  29.2 0.6 collective-permute-start.3
  29.8 0.0 collective-permute-done
  29.8 1.5 collective-permute-start.1
  31.3 2.6 %collective-permute-done.1 = bf16[1,12,1536]{2,1,0:T(8,128)(2,1)S(1)} collective-permute-done((bf16[1,12,1536]{2,1,0:T(8,128)(2,1)S(1)}, bf16[1,12,1536]{2,1,0:T(8,128)(2,1)S(1)}, u32[]{:S(2)}, u32[]{:S(2)}) %collective-permute-start.1) | collective-permute-done | bytes 36896 | tf_op jit(solution)/shard_map/ppermute | solution.py:50
  33.9 0.6 collective-permute-start.2
  34.5 3.4 %collective-permute-done.2 = bf16[1,12,1536]{2,1,0:T(8,128)(2,1)S(1)} collective-permute-done((bf16[1,12,1536]{2,1,0:T(8,128)(2,1)S(1)}, bf16[1,12,1536]{2,1,0:T(8,128)(2,1)S(1)}, u32[]{:S(2)}, u32[]{:S(2)}) %collective-permute-start.2) | collective-permute-done | bytes 36896 | tf_op jit(solution)/shard_map/ppermute | solution.py:50
  37.9 0.0 collective-permute-done.3
  37.9 0.0 collective-permute-done.4
  37.9 0.0 collective-permute-done.5
  38.0 0.0 collective-permute-done.6
  38.0 0.8 reshape.35
  38.8 0.0 all-gather.2.cloned.1.call-update
  38.8 0.0 reduce-scatter.2.cloned.1.call-start
  38.9 28.3 %all-gather.2.cloned.1.call-done = bf16[96,6144]{1,0:T(8,128)(2,1)} async-done(((bf16[96,1536]{1,0:T(8,128)(2,1)}), bf16[96,6144]{1,0:T(8,128)(2,1)}) %all-gather.2.cloned.1.call-update) | async-done | bytes 1179664 | tf_op jit(solution)/shard_map/all_gather | solution.py:57
  67.1 0.0 copy-start.2
  67.1 18.2 %fusion.2 = f32[96,3072]{1,0:T(8,128)S(1)} fusion(bf16[96,6144]{1,0:T(8,128)(2,1)} %all-gather.2.cloned.1.call-done, bf16[1,6144,3072]{2,1,0:T(8,128)(2,1)} %param.10), kind=kOutput, calls=%fused_computation.2 | convolution fusion | flops 3623878656 | bytes 40108032 | tf_op jit(solution)/shard_map/dot_general | solution.py:59
  85.4 0.0 copy-done.2
  85.4 28.1 %fusion.6 = bf16[96,6144]{1,0:T(8,128)(2,1)} fusion(bf16[1,3072,6144]{2,1,0:T(8,128)(2,1)} %param.11, f32[96,3072]{1,0:T(8,128)S(1)} %fusion.2, bf16[96,6144]{1,0:T(8,128)(2,1)S(1)} %copy-done.2, bf16[1,6144,3072]{2,1,0:T(8,128)(2,1)} %param.9), kind=kOutput, calls=%fused_computation.6 | convolution fusion | flops 7250116608 | bytes 79036416 | tf_op jit(solution)/shard_map/dot_general | solution.py:61
  113.5 0.0 reduce-scatter.2.cloned.1.call-update
  113.5 0.0 copy-start.1
  113.5 28.7 %reduce-scatter.2.cloned.1.call-done = bf16[96,1536]{1,0:T(8,128)(2,1)} async-done(((bf16[96,6144]{1,0:T(8,128)(2,1)}), bf16[96,1536]{1,0:T(8,128)(2,1)}) %reduce-scatter.2.cloned.1.call-update) | async-done | bytes 294928 | tf_op jit(solution)/shard_map/reduce_scatter | solution.py:62
  142.2 1.0 reshape.36
  143.2 11.8 %all_to_all.5 = bf16[8,12,1536]{2,1,0:T(8,128)(2,1)S(1)} all-to-all(bf16[8,12,1536]{2,1,0:T(8,128)(2,1)S(1)} %reshape.36), channel_id=1, replica_groups=mesh['dp'=8,'tensor'=4] {'dp'}, dimensions={0} | all-to-all | bytes 589824 | tf_op jit(solution)/shard_map/all_to_all | solution.py:64
  155.0 0.1 reshape.37
  155.0 0.9 convolution_convert_fusion.1
  155.9 0.0 copy-done.1
  (11 shorter events, 0.2 us)
Async XLA Ops:
  6.5 0.9 copy-start
  6.5 60.6 %all-gather.2.cloned.1.call-start = ((), (), s32[]{:S(2)}) async-start(), calls=%async_computation.2 | async-start | bytes 1474560 | tf_op jit(solution)/shard_map/all_gather | solution.py:57
  25.2 4.6 %collective-permute-start = (bf16[1,12,1536]{2,1,0:T(8,128)(2,1)S(1)}, bf16[1,12,1536]{2,1,0:T(8,128)(2,1)S(1)}, u32[]{:S(2)}, u32[]{:S(2)}) collective-permute-start(bf16[1,12,1536]{2,1,0:T(8,128)(2,1)S(1)} %get-tuple-element.15), channel_id=1, source_target_pairs={{0,4},{4,0},{8,12},{12,8},{16,20},{20,16},{24,28},{28,24},{1,5},{5... | collective-permute-start | bytes 110600 | tf_op jit(solution)/shard_map/ppermute | solution.py:50
  25.2 12.7 %collective-permute-start.6 = (bf16[1,12,1536]{2,1,0:T(8,128)(2,1)S(1)}, bf16[1,12,1536]{2,1,0:T(8,128)(2,1)S(1)}, u32[]{:S(2)}, u32[]{:S(2)}) collective-permute-start(bf16[1,12,1536]{2,1,0:T(8,128)(2,1)S(1)} %get-tuple-element.9), channel_id=1, source_target_pairs={{0,28},{4,24},{8,20},{12,16},{16,12},{20,8},{24,4},{28,0},{1,29},{... | collective-permute-start | bytes 110600 | tf_op jit(solution)/shard_map/ppermute | solution.py:50
  27.8 10.2 %collective-permute-start.5 = (bf16[1,12,1536]{2,1,0:T(8,128)(2,1)S(1)}, bf16[1,12,1536]{2,1,0:T(8,128)(2,1)S(1)}, u32[]{:S(2)}, u32[]{:S(2)}) collective-permute-start(bf16[1,12,1536]{2,1,0:T(8,128)(2,1)S(1)} %get-tuple-element.10), channel_id=1, source_target_pairs={{0,24},{4,28},{8,16},{12,20},{16,8},{20,12},{24,0},{28,4},{1,25},{... | collective-permute-start | bytes 110600 | tf_op jit(solution)/shard_map/ppermute | solution.py:50
  28.3 9.7 %collective-permute-start.4 = (bf16[1,12,1536]{2,1,0:T(8,128)(2,1)S(1)}, bf16[1,12,1536]{2,1,0:T(8,128)(2,1)S(1)}, u32[]{:S(2)}, u32[]{:S(2)}) collective-permute-start(bf16[1,12,1536]{2,1,0:T(8,128)(2,1)S(1)} %get-tuple-element.11), channel_id=1, source_target_pairs={{0,20},{4,16},{8,28},{12,24},{16,4},{20,0},{24,12},{28,8},{1,21},{... | collective-permute-start | bytes 110600 | tf_op jit(solution)/shard_map/ppermute | solution.py:50
  29.2 8.7 %collective-permute-start.3 = (bf16[1,12,1536]{2,1,0:T(8,128)(2,1)S(1)}, bf16[1,12,1536]{2,1,0:T(8,128)(2,1)S(1)}, u32[]{:S(2)}, u32[]{:S(2)}) collective-permute-start(bf16[1,12,1536]{2,1,0:T(8,128)(2,1)S(1)} %get-tuple-element.12), channel_id=1, source_target_pairs={{0,16},{4,20},{8,24},{12,28},{16,0},{20,4},{24,8},{28,12},{1,17},{... | collective-permute-start | bytes 110600 | tf_op jit(solution)/shard_map/ppermute | solution.py:50
  29.8 4.1 %collective-permute-start.1 = (bf16[1,12,1536]{2,1,0:T(8,128)(2,1)S(1)}, bf16[1,12,1536]{2,1,0:T(8,128)(2,1)S(1)}, u32[]{:S(2)}, u32[]{:S(2)}) collective-permute-start(bf16[1,12,1536]{2,1,0:T(8,128)(2,1)S(1)} %get-tuple-element.14), channel_id=1, source_target_pairs={{0,8},{4,12},{8,0},{12,4},{16,24},{20,28},{24,16},{28,20},{1,9},{5... | collective-permute-start | bytes 110600 | tf_op jit(solution)/shard_map/ppermute | solution.py:50
  33.9 4.0 %collective-permute-start.2 = (bf16[1,12,1536]{2,1,0:T(8,128)(2,1)S(1)}, bf16[1,12,1536]{2,1,0:T(8,128)(2,1)S(1)}, u32[]{:S(2)}, u32[]{:S(2)}) collective-permute-start(bf16[1,12,1536]{2,1,0:T(8,128)(2,1)S(1)} %get-tuple-element.13), channel_id=1, source_target_pairs={{0,12},{4,8},{8,4},{12,0},{16,28},{20,24},{24,20},{28,16},{1,13},{... | collective-permute-start | bytes 110600 | tf_op jit(solution)/shard_map/ppermute | solution.py:50
  38.8 103.4 %reduce-scatter.2.cloned.1.call-start = ((), (), s32[]{:S(2)}) async-start(), calls=%async_computation.3 | async-start | bytes 1474560 | tf_op jit(solution)/shard_map/reduce_scatter | solution.py:62
  67.1 18.2 %copy-start.2 = (bf16[96,6144]{1,0:T(8,128)(2,1)S(1)}, bf16[96,6144]{1,0:T(8,128)(2,1)}, u32[]{:S(2)}) copy-start(bf16[96,6144]{1,0:T(8,128)(2,1)} %all-gather.2.cloned.1.call-done) | copy-start | bytes 3538948
  113.5 42.5 %copy-start.1 = (bf16[32,1536]{1,0:T(8,128)(2,1)S(1)}, bf16[32,1536]{1,0:T(8,128)(2,1)}, u32[]{:S(2)}) copy-start(bf16[32,1536]{1,0:T(8,128)(2,1)} %param.6) | copy-start | bytes 294916
Sparse Core Ops, SparseCore 0:
  38.9 28.1 all-gather.1
  113.6 28.5 reduce-scatter.1
